TPU v7x, 32 devices: a whole 2x2x4 slice. The times are simulated.
32 devices in a mesh: row: 4 (over y, x), col: 8 (over z, core).
Axes of the slice: x: 2, y: 2, z: 4, core: 2. Of those that a mesh axis runs over, the one named last changes fastest.
Arguments:
- pair_window: bfloat16 [8, 16, 32, 128], P('col', 'row'), may hold values from -6 to 6
- tri_cotangent: bfloat16 [8, 16, 128, 128], P(None, 'row', 'col'), may hold values from -0.75 to 0.75
- saved_left: bfloat16 [8, 16, 32, 128], P('col', 'row'), may hold values from -6 to 6
- saved_right: bfloat16 [8, 16, 32, 128], P('col', 'row'), may hold values from -6 to 6
- norm_gain: float32 [128], replicated, may hold values from 0.5 to 1.5
- norm_bias: float32 [128], replicated, may hold values from -3 to 3
- proj_weight: bfloat16 [4, 128, 128], replicated, may hold values from -0.5 to 0.5
Outputs:
- pair_grad: bfloat16 [8, 16, 32, 128], P('col', 'row')
- weight_grad: float32 [4, 128, 128], replicated
- norm_grad: float32 [2, 128], replicated
All inputs are finite; a program needn't handle non-finite values.
Results may differ from a plain program's by a relative error of at most 0.0085.
Values may be sent and summed in bfloat16 or wider, within the bound.
A program may use at most 64 MiB of HBM per device.

v0:
```python
import jax
import jax.numpy as jnp
from jax import lax
from jax.sharding import PartitionSpec as P


def gated_norm_back(pair_rows, left_grad, right_grad, norm_gain, norm_bias, proj_weight):
    pair = pair_rows.astype(jnp.float32)
    average = jnp.mean(pair, axis=-1, keepdims=True)
    centred = pair - average
    variance = jnp.mean(centred * centred, axis=-1, keepdims=True)
    inv_std = lax.rsqrt(variance + 1e-05)
    unit_pair = centred * inv_std
    normed = (unit_pair * norm_gain + norm_bias).astype(jnp.bfloat16)
    chans = proj_weight.shape[2]
    stacked = jnp.transpose(proj_weight, (1, 0, 2)).reshape(proj_weight.shape[1], 4 * chans)
    preact = jnp.dot(normed, stacked, preferred_element_type=jnp.float32)
    gate_left = jax.nn.sigmoid(preact[:, :chans])
    value_left = preact[:, chans : 2 * chans]
    gate_right = jax.nn.sigmoid(preact[:, 2 * chans : 3 * chans])
    value_right = preact[:, 3 * chans :]
    pre_grads = jnp.concatenate(
        [
            left_grad * value_left * gate_left * (1.0 - gate_left),
            left_grad * gate_left,
            right_grad * value_right * gate_right * (1.0 - gate_right),
            right_grad * gate_right,
        ],
        axis=1,
    ).astype(jnp.bfloat16)
    weight_part = lax.dot_general(
        normed, pre_grads, (((0,), (0,)), ((), ())), preferred_element_type=jnp.float32
    )
    weight_part = jnp.transpose(weight_part.reshape(proj_weight.shape[1], 4, chans), (1, 0, 2))
    normed_grad = jnp.dot(pre_grads, stacked.T, preferred_element_type=jnp.float32)
    norm_part = jnp.stack([jnp.sum(normed_grad * unit_pair, axis=0), jnp.sum(normed_grad, axis=0)])
    scaled_grad = normed_grad * norm_gain
    pair_grad = inv_std * (
        scaled_grad
        - jnp.mean(scaled_grad, axis=-1, keepdims=True)
        - unit_pair * jnp.mean(scaled_grad * unit_pair, axis=-1, keepdims=True)
    )
    return (pair_grad.astype(jnp.bfloat16), weight_part, norm_part)


def on_device(
    pair_window, tri_cotangent, saved_left, saved_right, norm_gain, norm_bias, proj_weight
):
    block_count, own_rows, col_tokens, channels = tri_cotangent.shape
    window_len = saved_left.shape[2]
    right_rows = lax.all_gather(saved_right, "row", axis=1, tiled=True)[0]
    cot_flat = tri_cotangent.reshape(block_count * own_rows, col_tokens, channels)
    cot_piece = cot_flat
    left_grad = lax.psum_scatter(
        jnp.einsum("ijh,jkh->ikh", cot_piece, right_rows, preferred_element_type=jnp.float32),
        "col",
        scatter_dimension=0,
        tiled=True,
    )
    left_rows = lax.all_gather(saved_left, "col", axis=0, tiled=True)
    left_flat = left_rows.reshape(block_count * own_rows, window_len, channels)
    cot_piece = cot_flat
    right_grad = lax.psum_scatter(
        jnp.einsum("ijh,ikh->jkh", cot_piece, left_flat, preferred_element_type=jnp.float32),
        "row",
        scatter_dimension=0,
        tiled=True,
    )
    positions = own_rows * window_len
    pair_grad, weight_part, norm_part = gated_norm_back(
        pair_window.reshape(positions, pair_window.shape[3]),
        left_grad.reshape(positions, channels),
        right_grad.reshape(positions, channels),
        norm_gain,
        norm_bias,
        proj_weight,
    )
    weight_grad, norm_grad = lax.psum((weight_part, norm_part), ("row", "col"))
    return (pair_grad.reshape(pair_window.shape), weight_grad, norm_grad)


def solution(mesh):
    return jax.shard_map(
        on_device,
        mesh=mesh,
        in_specs=(
            P("col", "row", None, None),
            P(None, "row", "col", None),
            P("col", "row", None, None),
            P("col", "row", None, None),
            P(),
            P(),
            P(),
        ),
        out_specs=(P("col", "row", None, None), P(), P()),
        check_vma=False,
    )
```

profile of v0, /device:TPU:0, one launch (start us, length us, event | category | flops | bytes accessed | tf_op | source)
XLA Modules:
  0.0 225.6 jit_solution(12033966803922568109)
XLA Ops:
  7.2 1.4 copy.28
  8.6 16.1 %all_gather.7 = bf16[8,4,32,128]{3,2,1,0:T(8,128)(2,1)S(1)} all-gather(bf16[1,4,32,128]{3,2,1,0:T(8,128)(2,1)} %param.9), channel_id=1, replica_groups=mesh['row'=4,'col'=8] {'col'}, dimensions={0}, use_global_device_ids=true | all-gather | bytes 294912 | tf_op jit(solution)/shard_map/all_gather | solution.py:60
  24.8 0.9 copy.31
  25.7 0.4 convolution_bitcast_fusion.1
  26.1 1.1 copy.33
  27.3 8.5 %all_gather.6 = bf16[1,16,32,128]{3,2,0,1:T(8,128)(2,1)S(1)} all-gather(bf16[1,4,32,128]{3,2,0,1:T(8,128)(2,1)S(1)} %bitcast.59), channel_id=1, replica_groups=mesh['row'=4,'col'=8] {'row'}, dimensions={1}, use_global_device_ids=true | all-gather | bytes 163840 | tf_op jit(solution)/shard_map/all_gather | solution.py:51
  35.8 0.4 copy.27
  36.2 0.5 convolution_bitcast_fusion
  36.8 2.2 copy.29
  39.1 0.1 convert_reduce_fusion
  39.3 0.2 multiply_reduce_fusion.2
  39.6 0.1 copy.30
  39.7 0.1 add_convert_fusion
  39.8 0.2 fusion.19
  40.0 12.8 %reduce-scatter.5.cloned.1.call-done = f32[4,32,128]{2,1,0:T(8,128)} async-done(((f32[16,32,128]{2,1,0:T(8,128)}), f32[4,32,128]{2,1,0:T(8,128)}) %reduce-scatter.5.cloned.1.call-update) | async-done | bytes 65552 | tf_op jit(solution)/shard_map/reduce_scatter | solution.py:63
  52.8 33.6 %reduce-scatter.3.cloned.1.call-done = f32[4,32,128]{2,1,0:T(8,128)} async-done(((f32[32,32,128]{2,1,0:T(8,128)}), f32[4,32,128]{2,1,0:T(8,128)}) %reduce-scatter.3.cloned.1.call-update) | async-done | bytes 65552 | tf_op jit(solution)/shard_map/reduce_scatter | solution.py:54
  86.4 0.9 fusion.12
  87.4 0.1 copy.38
  87.5 0.9 convolution_bitcast_fusion.2
  88.4 0.3 multiply_reduce_fusion
  88.7 37.9 %psum.15 = f32[2,128]{1,0:T(2,128)} all-reduce(f32[2,128]{1,0:T(2,128)S(1)} %pad_maximum_fusion.2), channel_id=1, replica_groups=mesh['row'=4,'col'=8] {'row','col'}, use_global_device_ids=true, to_apply=%region_9.0 | all-reduce | flops 256 | bytes 2048 | tf_op jit(solution)/shard_map/psum | solution.py:78
  126.6 0.8 multiply_convert_fusion
  127.4 90.0 %all-reduce.2.cloned.1.call-done = f32[4,128,128]{2,1,0:T(8,128)} async-done(((f32[4,128,128]{2,1,0:T(8,128)}), f32[4,128,128]{2,1,0:T(8,128)}) %all-reduce.2.cloned.1.call-update) | async-done | bytes 262160 | tf_op jit(solution)/shard_map/psum | solution.py:78
  217.5 1.7 copy.40
  (23 shorter events, 0.4 us)
Async XLA Ops:
  7.2 45.6 %reduce-scatter.5.cloned.1.call-start = ((), (), s32[]{:S(2)}) async-start(), calls=%async_computation.3 | async-start | bytes 327680 | tf_op jit(solution)/shard_map/reduce_scatter | solution.py:63
  25.7 1.6 copy-start.2
  27.3 59.1 %reduce-scatter.3.cloned.1.call-start = ((), (), s32[]{:S(2)}) async-start(), calls=%async_computation.2 | async-start | bytes 589824 | tf_op jit(solution)/shard_map/reduce_scatter | solution.py:54
  36.8 2.3 %copy-start = (bf16[1,4,32,128]{3,2,1,0:T(8,128)(2,1)S(1)}, bf16[1,4,32,128]{3,2,1,0:T(8,128)(2,1)}, u32[]{:S(2)}) copy-start(bf16[1,4,32,128]{3,2,1,0:T(8,128)(2,1)} %param.7) | copy-start | bytes 98308
  36.8 2.8 %copy-start.1 = (bf16[4,128,128]{2,1,0:T(8,128)(2,1)S(1)}, bf16[4,128,128]{2,1,0:T(8,128)(2,1)}, u32[]{:S(2)}) copy-start(bf16[4,128,128]{2,1,0:T(8,128)(2,1)} %param.13) | copy-start | bytes 393220
  36.8 2.9 %copy-start.3 = (f32[128]{0:T(128)S(1)}, f32[128]{0:T(128)}, u32[]{:S(2)}) copy-start(f32[128]{0:T(128)} %param.11) | copy-start | bytes 1540
  36.8 2.9 %copy-start.4 = (f32[128]{0:T(128)S(1)}, f32[128]{0:T(128)}, u32[]{:S(2)}) copy-start(f32[128]{0:T(128)} %param.12) | copy-start | bytes 1540
  39.0 178.4 %all-reduce.2.cloned.1.call-start = ((), (), s32[]{:S(2)}) async-start(), calls=%async_computation.4 | async-start | bytes 524288 | tf_op jit(solution)/shard_map/psum | solution.py:78
Sparse Core Ops, SparseCore 0:
  27.4 25.3 reduce-scatter.4
  55.0 31.3 reduce-scatter.2
  92.5 124.9 all-reduce.1
where the time goes:
time: 226 us
  waiting for transfers between devices  136 us (60%)
  blocking collectives  62.5 us (28%)
  between operations  13.9 us (6%)
  local copies, waits for them, and re-layouts  8.23 us (4%)
  matrix products  2.3 us (1%)
    psum x1, waiting for transfers between devices, on_device(): weight_grad, norm_grad = lax.psum((weight_part, norm_part), ('row', 'col'))  90 us
    psum x1, blocking collectives, on_device(): weight_grad, norm_grad = lax.psum((weight_part, norm_part), ('row', 'col'))  37.9 us
    reduce_scatter x1, waiting for transfers between devices, on_device(): lax.psum_scatter(jnp.einsum('ijh,jkh->ikh', cot_piece, right_rows, prefer...  33.6 us
    all_gather x1, blocking collectives, on_device(): left_rows = lax.all_gather(saved_left, 'col', axis=0, tiled=True)  16.1 us
    reduce_scatter x1, waiting for transfers between devices, on_device(): lax.psum_scatter(jnp.einsum('ijh,ikh->jkh', cot_piece, left_flat, preferr...  12.8 us
    all_gather x1, blocking collectives, on_device(): right_rows = lax.all_gather(saved_right, 'row', axis=1, tiled=True)[0]  8.46 us
  transfers between devices with their start and end apart: 3, of which 3 were waited for; matrix products, arithmetic and copies ran while one was open for 2% of the time, Pallas kernels for 0%

commit v1 on v0

v1 whole, which is shorter than its diff:
```python
import functools

import jax
import jax.numpy as jnp
from jax import lax
from jax.experimental import pallas as pl
from jax.experimental.pallas import tpu as pltpu
from jax.sharding import PartitionSpec as P

MESH = pl.DeviceIdType.MESH
F32 = jnp.float32
BF16 = jnp.bfloat16


def kernel(
    R,
    C,
    fused,
    z_hbm,
    dt_hbm,
    a_hbm,
    b_hbm,
    gain_hbm,
    bias_hbm,
    w_hbm,
    pair_ref,
    wgrad_ref,
    norm_ref,
    z_ref,
    dt_ref,
    a_ref,
    b_ref,
    gain_ref,
    bias_ref,
    w_ref,
    dt_other,
    dtf,
    a_all,
    b_all,
    ga_send,
    gb_send,
    ga_all,
    gb_all,
    coef,
    xhat_ref,
    normt_ref,
    inv_ref,
    wsend,
    wrecv,
    wback,
    nrecv,
    in_sem,
    dt_sem,
    a_ssem,
    a_rsem,
    b_ssem,
    b_rsem,
    ga_ssem,
    ga_rsem,
    gb_ssem,
    gb_rsem,
    ws_ssem,
    ws_rsem,
    wb_ssem,
    wb_rsem,
    n_ssem,
    n_rsem,
):
    r, c = lax.axis_index("row"), lax.axis_index("col")
    Z, N = C // 2, R * C
    z, q = c // 2, c % 2
    me = r * C + c
    T = a_ref.shape[1]
    K, H = a_ref.shape[2], a_ref.shape[3]
    KH = K // 2
    J = R * T

    def where(d):
        return (d // C, d % C)

    col_peers = [(s, lax.rem(c + s, C)) for s in range(1, C)]
    row_peers = [lax.rem(r + s, R) for s in range(1, R)]

    barrier = pltpu.get_barrier_semaphore()
    if fused:
        for s in range(1, N):
            pl.semaphore_signal(barrier, 1, device_id=where(lax.rem(me + s, N)), device_id_type=MESH)
        expected = N - 1
    else:
        for _, cc in col_peers:
            pl.semaphore_signal(barrier, 1, device_id=(r, cc), device_id_type=MESH)
        for rr in row_peers:
            for p in range(2):
                pl.semaphore_signal(barrier, 1, device_id=(rr, z * 2 + p), device_id_type=MESH)
        expected = C - 1 + 2 * (R - 1)

    loads = []
    for n, (src, dst) in enumerate(
        (
            (a_hbm, a_ref),
            (b_hbm, b_ref),
            (dt_hbm, dt_ref),
            (z_hbm, z_ref),
            (gain_hbm, gain_ref),
            (bias_hbm, bias_ref),
            (w_hbm, w_ref),
        )
    ):
        load = pltpu.make_async_copy(src, dst, in_sem.at[n])
        load.start()
        loads.append(load)
    for load in loads[:3]:
        load.wait()
    pl.semaphore_wait(barrier, expected)

    def remote(src, dst, ssem, rsem, dev):
        return pltpu.make_async_remote_copy(
            src_ref=src, dst_ref=dst, send_sem=ssem, recv_sem=rsem, device_id=dev, device_id_type=MESH
        )

    other = z * 2 + (1 - q)

    def half(p):
        return pl.ds(p * KH if isinstance(p, int) else pl.multiple_of(p * KH, KH), KH)

    sends = []

    def push(copy):
        copy.start()
        sends.append(copy)

    push(remote(dt_ref, dt_other, dt_sem.at[0], dt_sem.at[1], (r, other)))
    push(remote(b_ref.at[0, :, half(1 - q), :], b_all.at[q, pl.ds(r * T, T)], b_ssem.at[r, 1 - q], b_rsem.at[r, q], (r, other)))
    for rr in row_peers:
        for p in range(2):
            push(remote(b_ref.at[0, :, half(p), :], b_all.at[q, pl.ds(r * T, T)], b_ssem.at[rr, p], b_rsem.at[r, q], (rr, z * 2 + p)))
    for s in range(1, Z):
        zz = lax.rem(z + s, Z)
        for p in range(2):
            push(remote(a_ref.at[0, :, half(p), :], a_all.at[pl.ds(c * T, T)], a_ssem.at[zz * 2 + p], a_rsem.at[c], (r, zz * 2 + p)))
    push(remote(a_ref.at[0, :, half(1 - q), :], a_all.at[pl.ds(c * T, T)], a_ssem.at[other], a_rsem.at[c], (r, other)))

    for t in range(T):
        a_all[c * T + t] = a_ref[0, t, half(q), :]
        b_all[q, r * T + t] = b_ref[0, t, half(q), :]
    dtf[q] = dt_ref[...].reshape(C * T, J, H).astype(F32)

    for load in loads[3:]:
        load.wait()
    pair = z_ref[...].reshape(T * K, H).astype(F32)
    average = jnp.mean(pair, axis=-1, keepdims=True)
    centred = pair - average
    variance = jnp.mean(centred * centred, axis=-1, keepdims=True)
    inv_std = lax.rsqrt(variance + 1e-05)
    xhat = centred * inv_std
    normed32 = xhat * gain_ref[...] + bias_ref[...]
    normed = normed32.astype(BF16)
    normt_ref[...] = jnp.transpose(normed32).astype(BF16)
    xhat_ref[...] = xhat
    inv_ref[...] = jnp.broadcast_to(inv_std, inv_ref.shape)
    for m in range(2):
        gate = jax.nn.sigmoid(jnp.dot(normed, w_ref[2 * m], preferred_element_type=F32))
        value = jnp.dot(normed, w_ref[2 * m + 1], preferred_element_type=F32)
        coef[2 * m] = value * gate * (1.0 - gate)
        coef[2 * m + 1] = gate

    remote(dt_ref, dt_other, dt_sem.at[0], dt_sem.at[1], (r, other)).wait_recv()
    dtf[1 - q] = dt_other[...].reshape(C * T, J, H).astype(F32)

    def b_wait(rr, p):
        remote(b_all.at[p, pl.ds(rr * T, T)], b_all.at[p, pl.ds(rr * T, T)], b_ssem.at[rr, p], b_rsem.at[rr, p], (r, other)).wait_recv()

    b_wait(r, 1 - q)
    for rr in row_peers:
        for p in range(2):
            b_wait(rr, p)

    zero = jnp.zeros((KH, H), F32)
    for s in list(range(1, Z)) + [0]:
        zz = lax.rem(z + s, Z)
        acc = (zero,) * (2 * T)
        for core in range(2):

            def step(j, acc, core=core, zz=zz):
                right = b_all[core, j].astype(F32)
                return tuple(
                    acc[n] + dtf[core, zz * 2 * T + n, pl.ds(j, 1), :] * right for n in range(2 * T)
                )

            acc = lax.fori_loop(0, J, step, acc, unroll=4)
        if s:
            for p in range(2):
                for t in range(T):
                    ga_send[s, p, t] = acc[p * T + t].astype(BF16)
                push(remote(ga_send.at[s, p], ga_all.at[z, q], ga_ssem.at[s, p], ga_rsem.at[z, q], (r, zz * 2 + p)))
        else:
            for t in range(T):
                keep = jnp.where(q == 0, acc[t], acc[T + t])
                give = jnp.where(q == 0, acc[T + t], acc[t])
                ga_send[0, 0, t] = give.astype(BF16)
                ga_all[z, q, t] = keep.astype(BF16)
            push(remote(ga_send.at[0, 0], ga_all.at[z, q], ga_ssem.at[0, 0], ga_rsem.at[z, q], (r, other)))

    def a_wait(cc):
        remote(a_all.at[pl.ds(cc * T, T)], a_all.at[pl.ds(cc * T, T)], a_ssem.at[cc], a_rsem.at[cc], (r, other)).wait_recv()

    for _, cc in col_peers:
        a_wait(cc)
    for s in list(range(1, R)) + [0]:
        rr = lax.rem(r + s, R)

        def step(i, acc, rr=rr):
            left = a_all[i].astype(F32)
            return tuple(
                acc[n] + dtf[n // T, i, pl.ds(rr * T + n % T, 1), :] * left for n in range(2 * T)
            )

        acc = lax.fori_loop(0, C * T, step, (zero,) * (2 * T), unroll=4)
        if s:
            for p in range(2):
                for t in range(T):
                    gb_send[s, p, t] = acc[p * T + t].astype(BF16)
                push(remote(gb_send.at[s, p], gb_all.at[r, q], gb_ssem.at[s, p], gb_rsem.at[r, q], (rr, z * 2 + p)))
        else:
            for t in range(T):
                keep = jnp.where(q == 0, acc[t], acc[T + t])
                give = jnp.where(q == 0, acc[T + t], acc[t])
                gb_send[0, 0, t] = give.astype(BF16)
                gb_all[r, q, t] = keep.astype(BF16)
            push(remote(gb_send.at[0, 0], gb_all.at[r, q], gb_ssem.at[0, 0], gb_rsem.at[r, q], (r, other)))

    def total(buf, count):
        rows = []
        for t in range(T):
            for p in range(2):
                acc = buf[0, p, t].astype(F32)
                for n in range(1, count):
                    acc = acc + buf[n, p, t].astype(F32)
                rows.append(acc)
        return jnp.concatenate(rows, axis=0)

    def slot_wait(buf, sem, n, p):
        remote(buf.at[n, p], buf.at[n, p], dt_sem.at[0], sem.at[n, p], (r, other)).wait_recv()

    chunk = 4 * H // N if fused else 0
    normt = normt_ref[...]

    def weight_part(m, g):
        part = jnp.dot(normt, g, preferred_element_type=F32)
        if fused:
            per = part.shape[0] // chunk
            wsend[m * per : (m + 1) * per] = part.astype(BF16).reshape(per, chunk, H)
        else:
            wgrad_ref[m] = part

    def dn_part(m, g):
        return lax.dot_general(g, w_ref[m], (((1,), (1,)), ((), ())), preferred_element_type=F32)

    for s in list(range(1, Z)):
        zz = lax.rem(z + s, Z)
        for p in range(2):
            slot_wait(ga_all, ga_rsem, zz, p)
    slot_wait(ga_all, ga_rsem, z, 1 - q)
    left_grad = total(ga_all, Z)
    g = [(left_grad * coef[m]).astype(BF16) for m in range(2)]
    weight_part(0, g[0])
    weight_part(1, g[1])
    dn = dn_part(0, g[0]) + dn_part(1, g[1])

    for s in list(range(1, R)):
        rr = lax.rem(r + s, R)
        for p in range(2):
            slot_wait(gb_all, gb_rsem, rr, p)
    slot_wait(gb_all, gb_rsem, r, 1 - q)
    right_grad = total(gb_all, R)
    g = [(right_grad * coef[m]).astype(BF16) for m in range(2, 4)]
    weight_part(2, g[0])
    weight_part(3, g[1])
    if fused:
        for s in range(1, N):
            d = lax.rem(me + s, N)
            push(remote(wsend.at[d], wrecv.at[me], ws_ssem.at[s], ws_rsem.at[me], where(d)))
        wrecv[me] = wsend[me]
    dn = dn + dn_part(2, g[0]) + dn_part(3, g[1])

    xhat = xhat_ref[...]
    norm_part = jnp.concatenate(
        [jnp.sum(dn * xhat, axis=0, keepdims=True), jnp.sum(dn, axis=0, keepdims=True)], axis=0
    )
    if fused:
        nrecv[me] = norm_part
        for s in range(1, N):
            d = lax.rem(me + s, N)
            push(remote(nrecv.at[me], nrecv.at[me], n_ssem.at[s], n_rsem.at[me], where(d)))
    else:
        norm_ref[...] = norm_part
    dh = dn * gain_ref[...]
    grad = inv_ref[...] * (
        dh
        - jnp.mean(dh, axis=-1, keepdims=True)
        - xhat * jnp.mean(dh * xhat, axis=-1, keepdims=True)
    )
    pair_ref[...] = grad.astype(BF16).reshape(pair_ref.shape)

    if fused:
        for s in range(1, N):
            d = lax.rem(me + s, N)
            remote(wrecv.at[d], wrecv.at[d], ws_ssem.at[s], ws_rsem.at[d], where(d)).wait_recv()
        acc = wrecv[0].astype(F32)
        for n in range(1, N):
            acc = acc + wrecv[n].astype(F32)
        wback[me] = acc.astype(BF16)
        for s in range(1, N):
            d = lax.rem(me + s, N)
            push(remote(wback.at[me], wback.at[me], wb_ssem.at[s], wb_rsem.at[me], where(d)))
        for s in range(1, N):
            d = lax.rem(me + s, N)
            remote(nrecv.at[d], nrecv.at[d], n_ssem.at[s], n_rsem.at[d], where(d)).wait_recv()
        acc = nrecv[0]
        for n in range(1, N):
            acc = acc + nrecv[n]
        norm_ref[...] = acc
        for s in range(1, N):
            d = lax.rem(me + s, N)
            remote(wback.at[d], wback.at[d], wb_ssem.at[s], wb_rsem.at[d], where(d)).wait_recv()
        wgrad_ref[...] = wback[...].astype(F32).reshape(wgrad_ref.shape)
    for copy in sends:
        copy.wait_send()


def on_device(R, C, z, dt, a, b, gain, bias, w):
    _, T, K, H = a.shape
    J = dt.shape[2]
    KH, Z, N = K // 2, C // 2, R * C
    fused = (4 * H) % (16 * N) == 0
    M = N if fused else 1
    chunk = 4 * H // N if fused else 16
    V = pltpu.VMEM
    D = pltpu.SemaphoreType.DMA
    anyspace = pl.BlockSpec(memory_space=pl.ANY)
    vspace = pl.BlockSpec(memory_space=pltpu.VMEM)
    pair, wgrad, norm = pl.pallas_call(
        functools.partial(kernel, R, C, fused),
        out_shape=(
            jax.ShapeDtypeStruct(z.shape, BF16),
            jax.ShapeDtypeStruct(w.shape, F32),
            jax.ShapeDtypeStruct((2, z.shape[3]), F32),
        ),
        in_specs=[anyspace] * 7,
        out_specs=(vspace,) * 3,
        scratch_shapes=[
            V(z.shape, BF16),
            V(dt.shape, BF16),
            V(a.shape, BF16),
            V(b.shape, BF16),
            V((1, H), F32),
            V((1, H), F32),
            V(w.shape, BF16),
            V(dt.shape, BF16),
            V((2, C * T, J, H), F32),
            V((C * T, KH, H), BF16),
            V((2, J, KH, H), BF16),
            V((Z, 2, T, KH, H), BF16),
            V((R, 2, T, KH, H), BF16),
            V((Z, 2, T, KH, H), BF16),
            V((R, 2, T, KH, H), BF16),
            V((4, T * K, H), F32),
            V((T * K, H), F32),
            V((H, T * K), BF16),
            V((T * K, H), F32),
            V((M, chunk, H), BF16),
            V((M, chunk, H), BF16),
            V((M, chunk, H), BF16),
            V((M, 2, H), F32),
            D((7,)),
            D((2,)),
            D((C,)),
            D((C,)),
            D((R, 2)),
            D((R, 2)),
            D((Z, 2)),
            D((Z, 2)),
            D((R, 2)),
            D((R, 2)),
            D((M,)),
            D((M,)),
            D((M,)),
            D((M,)),
            D((M,)),
            D((M,)),
        ],
        compiler_params=pltpu.CompilerParams(
            collective_id=0, has_side_effects=True, vmem_limit_bytes=56 * 1024 * 1024
        ),
    )(z, dt, a, b, gain.reshape(1, -1), bias.reshape(1, -1), w)
    if not fused:
        wgrad, norm = lax.psum((wgrad, norm), ("row", "col"))
    return pair, wgrad, norm


def solution(mesh):
    R, C = mesh.shape["row"], mesh.shape["col"]
    return jax.shard_map(
        functools.partial(on_device, R, C),
        mesh=mesh,
        in_specs=(
            P("col", "row", None, None),
            P(None, "row", "col", None),
            P("col", "row", None, None),
            P("col", "row", None, None),
            P(),
            P(),
            P(),
        ),
        out_specs=(P("col", "row", None, None), P(), P()),
        check_vma=False,
    )
```

time: 226 us -> 34.4 us (0.15)
  waiting for transfers between devices: 136 us -> 0 us
  blocking collectives: 62.5 us -> 0 us
  Pallas kernels: 0 us -> 29.9 us
  between operations: 13.9 us -> 0.64 us
  local copies, waits for them, and re-layouts: 8.23 us -> 3.61 us
  matrix products: 2.3 us -> 0 us
    psum x1 -> x0, waiting for transfers between devices: 90 us -> none  [on_device(): weight_grad, norm_grad = lax.psum((weight_part, norm_part), ('row', 'col'))]
    reduce_scatter x2 -> x0, waiting for transfers between devices: 46.4 us -> none  [the longest x1 33.6 us: on_device(): lax.psum_scatter(jnp.einsum('ijh,jkh->ikh', cot_piece, right_rows, prefer...]
    psum x1 -> x0, blocking collectives: 37.9 us -> none  [on_device(): weight_grad, norm_grad = lax.psum((weight_part, norm_part), ('row', 'col'))]
    pallas_call x0 -> x1, Pallas kernels: none -> 29.9 us  [on_device(): pl.pallas_call(functools.partial(kernel, R, C, fused), out_shape=(jax.Sha...]
    all_gather x2 -> x0, blocking collectives: 24.6 us -> none  [the longest x1 16.1 us: on_device(): left_rows = lax.all_gather(saved_left, 'col', axis=0, tiled=True)]
    transpose x2 -> x0, local copies, waits for them, and re-layouts: 3.33 us -> none  [the longest x1 2.21 us: on_device(): jnp.einsum('ijh,jkh->ikh', cot_piece, right_rows, preferred_element_type=...]
    dot_general x5 -> x0, matrix products: 2.3 us -> none  [the longest x1 0.92 us: gated_norm_back(): lax.dot_general(normed, pre_grads, (((0,), (0,)), ((), ())), preferred_el...]
  transfers between devices with their start and end apart: 3 -> 0, of which waited for: 3 -> 0; matrix products, arithmetic and copies ran while one was open for 2% -> 0% of each run, Pallas kernels for 0% -> 0%
where the time goes in v1:
time: 34.4 us; the launch traced here: 34.2 us
  Pallas kernels  29.9 us (87%)
  local copies, waits for them, and re-layouts  3.61 us (10%)
  between operations  0.64 us (2%)
    pallas_call x1, Pallas kernels, on_device(): pl.pallas_call(functools.partial(kernel, R, C, fused), out_shape=(jax.Sha...  29.9 us
    unnamed x5, local copies, waits for them, and re-layouts  3.61 us

profile of v1, /device:TPU:0, one launch (start us, length us, event | category | flops | bytes accessed | tf_op | source)
XLA Modules:
  0.0 34.2 jit_solution(13044291169667530035)
XLA Ops:
  0.6 29.9 %shard_map.94 = (bf16[1,4,32,128]{3,2,1,0:T(8,128)(2,1)}, f32[4,128,128]{2,1,0:T(8,128)}, f32[2,128]{1,0:T(2,128)}) custom-call(bf16[1,4,32,128]{3,2,1,0:T(8,128)(2,1)} %z_hbm.1, bf16[8,4,16,128]{3,2,1,0:T(8,128)(2,1)} %dt_hbm.1, bf16[1,4,32,128]{3,2,1,0:T(8,128)(2,1)} %a_hbm.1, bf16[1,4,32,128]{3,2,1,0:T(8,128)(2,1)} %b_hbm.1, f32[1,128]{1,0:T(1,128)} %bitcast.2, ...), custom_call_target="tpu_custom_call" | custom-call | tf_op jit(solution)/shard_map/pallas_call | solution.py:342
  30.6 1.4 %copy.13 = bf16[1,4,32,128]{3,2,1,0:T(8,128)(2,1)} copy(bf16[1,4,32,128]{3,2,1,0:T(8,128)(2,1)} %get-tuple-element.6) | data formatting | bytes 65536
  31.9 0.0 copy-start
  31.9 1.7 %copy.14 = f32[4,128,128]{2,1,0:T(8,128)} copy(f32[4,128,128]{2,1,0:T(8,128)} %get-tuple-element.7) | data formatting | bytes 524288
  33.6 0.0 copy-done
  33.6 0.6 %copy.15 = f32[2,128]{1,0:T(2,128)} copy(f32[2,128]{1,0:T(2,128)S(1)} %copy-done) | data formatting | bytes 2048
Async XLA Ops:
  31.9 1.7 %copy-start = (f32[2,128]{1,0:T(2,128)S(1)}, f32[2,128]{1,0:T(2,128)}, u32[]{:S(2)}) copy-start(f32[2,128]{1,0:T(2,128)} %get-tuple-element.8) | copy-start | bytes 3076

commit v2 on v1

--- a/solution.py
+++ b/solution.py
@@ -242,16 +242,35 @@
     def slot_wait(buf, sem, n, p):
         remote(buf.at[n, p], buf.at[n, p], dt_sem.at[0], sem.at[n, p], (r, other)).wait_recv()
 
-    chunk = 4 * H // N if fused else 0
+    chunk = 2 * H // N if fused else 0
     normt = normt_ref[...]
 
     def weight_part(m, g):
         part = jnp.dot(normt, g, preferred_element_type=F32)
         if fused:
             per = part.shape[0] // chunk
-            wsend[m * per : (m + 1) * per] = part.astype(BF16).reshape(per, chunk, H)
+            at = (m % 2) * per
+            wsend[m // 2, at : at + per] = part.astype(BF16).reshape(per, chunk, H)
         else:
             wgrad_ref[m] = part
+
+    def spread(side):
+        for s in range(1, N):
+            d = lax.rem(me + s, N)
+            push(remote(wsend.at[side, d], wrecv.at[side, me], ws_ssem.at[side, s], ws_rsem.at[side, me], where(d)))
+        wrecv[side, me] = wsend[side, me]
+
+    def collect(side):
+        for s in range(1, N):
+            d = lax.rem(me + s, N)
+            remote(wrecv.at[side, d], wrecv.at[side, d], ws_ssem.at[side, s], ws_rsem.at[side, d], where(d)).wait_recv()
+        acc = wrecv[side, 0].astype(F32)
+        for n in range(1, N):
+            acc = acc + wrecv[side, n].astype(F32)
+        wback[side, me] = acc.astype(BF16)
+        for s in range(1, N):
+            d = lax.rem(me + s, N)
+            push(remote(wback.at[side, me], wback.at[side, me], wb_ssem.at[side, s], wb_rsem.at[side, me], where(d)))
 
     def dn_part(m, g):
         return lax.dot_general(g, w_ref[m], (((1,), (1,)), ((), ())), preferred_element_type=F32)
@@ -265,6 +284,8 @@
     g = [(left_grad * coef[m]).astype(BF16) for m in range(2)]
     weight_part(0, g[0])
     weight_part(1, g[1])
+    if fused:
+        spread(0)
     dn = dn_part(0, g[0]) + dn_part(1, g[1])
 
     for s in list(range(1, R)):
@@ -277,10 +298,7 @@
     weight_part(2, g[0])
     weight_part(3, g[1])
     if fused:
-        for s in range(1, N):
-            d = lax.rem(me + s, N)
-            push(remote(wsend.at[d], wrecv.at[me], ws_ssem.at[s], ws_rsem.at[me], where(d)))
-        wrecv[me] = wsend[me]
+        spread(1)
     dn = dn + dn_part(2, g[0]) + dn_part(3, g[1])
 
     xhat = xhat_ref[...]
@@ -303,16 +321,8 @@
     pair_ref[...] = grad.astype(BF16).reshape(pair_ref.shape)
 
     if fused:
-        for s in range(1, N):
-            d = lax.rem(me + s, N)
-            remote(wrecv.at[d], wrecv.at[d], ws_ssem.at[s], ws_rsem.at[d], where(d)).wait_recv()
-        acc = wrecv[0].astype(F32)
-        for n in range(1, N):
-            acc = acc + wrecv[n].astype(F32)
-        wback[me] = acc.astype(BF16)
-        for s in range(1, N):
-            d = lax.rem(me + s, N)
-            push(remote(wback.at[me], wback.at[me], wb_ssem.at[s], wb_rsem.at[me], where(d)))
+        collect(0)
+        collect(1)
         for s in range(1, N):
             d = lax.rem(me + s, N)
             remote(nrecv.at[d], nrecv.at[d], n_ssem.at[s], n_rsem.at[d], where(d)).wait_recv()
@@ -322,10 +332,26 @@
         norm_ref[...] = acc
         for s in range(1, N):
             d = lax.rem(me + s, N)
-            remote(wback.at[d], wback.at[d], wb_ssem.at[s], wb_rsem.at[d], where(d)).wait_recv()
-        wgrad_ref[...] = wback[...].astype(F32).reshape(wgrad_ref.shape)
+            for side in range(2):
+                remote(wback.at[side, d], wback.at[side, d], wb_ssem.at[side, s], wb_rsem.at[side, d], where(d)).wait_recv()
+        wgrad_ref[...] = wback[...].reshape(wgrad_ref.shape)
     for copy in sends:
         copy.wait_send()
+
+
+def finish(pair_ref, wgrad_ref, norm_ref, pair_out, wgrad_out, norm_out, wide, sem):
+    copies = [
+        pltpu.make_async_copy(pair_ref, pair_out, sem.at[0]),
+        pltpu.make_async_copy(norm_ref, norm_out, sem.at[1]),
+    ]
+    for copy in copies:
+        copy.start()
+    for m in range(wide.shape[0]):
+        wide[m] = wgrad_ref[m].astype(F32)
+        copies.append(pltpu.make_async_copy(wide.at[m], wgrad_out.at[m], sem.at[2 + m]))
+        copies[-1].start()
+    for copy in copies:
+        copy.wait()
 
 
 def on_device(R, C, z, dt, a, b, gain, bias, w):
@@ -334,7 +360,7 @@
     KH, Z, N = K // 2, C // 2, R * C
     fused = (4 * H) % (16 * N) == 0
     M = N if fused else 1
-    chunk = 4 * H // N if fused else 16
+    chunk = 2 * H // N if fused else 8
     V = pltpu.VMEM
     D = pltpu.SemaphoreType.DMA
     anyspace = pl.BlockSpec(memory_space=pl.ANY)
@@ -342,9 +368,9 @@
     pair, wgrad, norm = pl.pallas_call(
         functools.partial(kernel, R, C, fused),
         out_shape=(
-            jax.ShapeDtypeStruct(z.shape, BF16),
-            jax.ShapeDtypeStruct(w.shape, F32),
-            jax.ShapeDtypeStruct((2, z.shape[3]), F32),
+            pltpu.VMEM(z.shape, BF16),
+            pltpu.VMEM(w.shape, BF16 if fused else F32),
+            pltpu.VMEM((2, z.shape[3]), F32),
         ),
         in_specs=[anyspace] * 7,
         out_specs=(vspace,) * 3,
@@ -368,9 +394,9 @@
             V((T * K, H), F32),
             V((H, T * K), BF16),
             V((T * K, H), F32),
-            V((M, chunk, H), BF16),
-            V((M, chunk, H), BF16),
-            V((M, chunk, H), BF16),
+            V((2, M, chunk, H), BF16),
+            V((2, M, chunk, H), BF16),
+            V((2, M, chunk, H), BF16),
             V((M, 2, H), F32),
             D((7,)),
             D((2,)),
@@ -382,10 +408,10 @@
             D((Z, 2)),
             D((R, 2)),
             D((R, 2)),
-            D((M,)),
-            D((M,)),
-            D((M,)),
-            D((M,)),
+            D((2, M)),
+            D((2, M)),
+            D((2, M)),
+            D((2, M)),
             D((M,)),
             D((M,)),
         ],
@@ -395,7 +421,18 @@
     )(z, dt, a, b, gain.reshape(1, -1), bias.reshape(1, -1), w)
     if not fused:
         wgrad, norm = lax.psum((wgrad, norm), ("row", "col"))
-    return pair, wgrad, norm
+    return pl.pallas_call(
+        finish,
+        out_shape=(
+            jax.ShapeDtypeStruct(z.shape, BF16),
+            jax.ShapeDtypeStruct(w.shape, F32),
+            jax.ShapeDtypeStruct(norm.shape, F32),
+        ),
+        in_specs=[vspace] * 3,
+        out_specs=(anyspace,) * 3,
+        scratch_shapes=[V(w.shape, F32), D((2 + w.shape[0],))],
+        compiler_params=pltpu.CompilerParams(vmem_limit_bytes=4 * 1024 * 1024),
+    )(pair, wgrad, norm)
 
 
 def solution(mesh):

time: 34.4 us -> 31.4 us (0.913)
  local copies, waits for them, and re-layouts: 3.61 us -> 0 us
  Pallas kernels: 29.9 us -> 30.6 us
    unnamed x5 -> x0, local copies, waits for them, and re-layouts: 3.61 us -> none
    pallas_call x1 -> x2, Pallas kernels: 29.9 us -> 30.6 us  [the longest x1 29.8 us: on_device(): pl.pallas_call(functools.partial(kernel, R, C, fused), out_shape=(pltpu.V...]
where the time goes in v2:
time: 31.4 us; the launch traced here: 31.2 us
  Pallas kernels  30.6 us (97%)
  between operations  0.64 us (2%)
    pallas_call x1, Pallas kernels, on_device(): pl.pallas_call(functools.partial(kernel, R, C, fused), out_shape=(pltpu.V...  29.8 us
    pallas_call x1, Pallas kernels, on_device(): pl.pallas_call(finish, out_shape=(jax.ShapeDtypeStruct(z.shape, BF16), ja...  0.76 us

profile of v2, /device:TPU:0, one launch (start us, length us, event | category | flops | bytes accessed | tf_op | source)
XLA Modules:
  0.0 31.2 jit_solution(13167248686174547043)
XLA Ops:
  0.6 29.8 %shard_map.94 = (bf16[1,4,32,128]{3,2,1,0:T(8,128)(2,1)S(1)}, bf16[4,128,128]{2,1,0:T(8,128)(2,1)S(1)}, f32[2,128]{1,0:T(2,128)S(1)}) custom-call(bf16[1,4,32,128]{3,2,1,0:T(8,128)(2,1)} %z_hbm.1, bf16[8,4,16,128]{3,2,1,0:T(8,128)(2,1)} %dt_hbm.1, bf16[1,4,32,128]{3,2,1,0:T(8,128)(2,1)} %a_hbm.1, bf16[1,4,32,128]{3,2,1,0:T(8,128)(2,1)} %b_hbm.1, ...), custom_call_target="tpu_custom_call" | custom-call | tf_op jit(solution)/shard_map/pallas_call | solution.py:368
  30.4 0.8 %shard_map.95 = (bf16[1,4,32,128]{3,2,1,0:T(8,128)(2,1)}, f32[4,128,128]{2,1,0:T(8,128)}, f32[2,128]{1,0:T(2,128)}) custom-call(bf16[1,4,32,128]{3,2,1,0:T(8,128)(2,1)S(1)} %get-tuple-element.6.pair_ref, bf16[4,128,128]{2,1,0:T(8,128)(2,1)S(1)} %get-tuple-element.7.wgrad_ref, f32[2,128]{1,0:T(2,128)S(1)} %get-tuple-element.8.norm_ref), custom_call_target="tpu_custom_call" | custom-call | tf_op jit(solution)/shard_map/pallas_call | solution.py:424

commit v3 on v2

--- a/solution.py
+++ b/solution.py
@@ -82,17 +82,12 @@
     row_peers = [lax.rem(r + s, R) for s in range(1, R)]
 
     barrier = pltpu.get_barrier_semaphore()
-    if fused:
-        for s in range(1, N):
-            pl.semaphore_signal(barrier, 1, device_id=where(lax.rem(me + s, N)), device_id_type=MESH)
-        expected = N - 1
-    else:
-        for _, cc in col_peers:
-            pl.semaphore_signal(barrier, 1, device_id=(r, cc), device_id_type=MESH)
-        for rr in row_peers:
-            for p in range(2):
-                pl.semaphore_signal(barrier, 1, device_id=(rr, z * 2 + p), device_id_type=MESH)
-        expected = C - 1 + 2 * (R - 1)
+    for _, cc in col_peers:
+        pl.semaphore_signal(barrier, 1, device_id=(r, cc), device_id_type=MESH)
+    for rr in row_peers:
+        for p in range(2):
+            pl.semaphore_signal(barrier, 1, device_id=(rr, z * 2 + p), device_id_type=MESH)
+    expected = C - 1 + 2 * (R - 1)
 
     loads = []
     for n, (src, dst) in enumerate(
@@ -242,7 +237,19 @@
     def slot_wait(buf, sem, n, p):
         remote(buf.at[n, p], buf.at[n, p], dt_sem.at[0], sem.at[n, p], (r, other)).wait_recv()
 
-    chunk = 2 * H // N if fused else 0
+    O = 2 * R
+    chunk = 2 * H // O if fused else 0
+    mid = Z // 2
+    nearest = r * 2 + jnp.where(z >= mid, 1, 0)
+    is_owner = (q == 1) & ((z == mid - 1) | (z == mid))
+
+    def owner_device(o):
+        return (o // 2, (mid - 1 + o % 2) * 2 + 1)
+
+    def await_all(buf, count, ssem, rsem):
+        part = buf.at[pl.ds(0, count)]
+        return remote(part, part, ssem, rsem, (r, other))
+
     normt = normt_ref[...]
 
     def weight_part(m, g):
@@ -255,22 +262,27 @@
             wgrad_ref[m] = part
 
     def spread(side):
-        for s in range(1, N):
-            d = lax.rem(me + s, N)
-            push(remote(wsend.at[side, d], wrecv.at[side, me], ws_ssem.at[side, s], ws_rsem.at[side, me], where(d)))
-        wrecv[side, me] = wsend[side, me]
+        for s in range(1, O):
+            o = lax.rem(nearest + s, O)
+            remote(wsend.at[side, o], wrecv.at[side, me], ws_ssem.at[side], ws_rsem.at[side], owner_device(o)).start()
+
+        @pl.when(is_owner)
+        def _():
+            wrecv[side, me] = wsend[side, nearest]
+
+        @pl.when(jnp.logical_not(is_owner))
+        def _():
+            remote(wsend.at[side, nearest], wrecv.at[side, me], ws_ssem.at[side], ws_rsem.at[side], owner_device(nearest)).start()
 
     def collect(side):
-        for s in range(1, N):
-            d = lax.rem(me + s, N)
-            remote(wrecv.at[side, d], wrecv.at[side, d], ws_ssem.at[side, s], ws_rsem.at[side, d], where(d)).wait_recv()
+        await_all(wrecv.at[side], N - 1, ws_ssem.at[side], ws_rsem.at[side]).wait_recv()
         acc = wrecv[side, 0].astype(F32)
         for n in range(1, N):
             acc = acc + wrecv[side, n].astype(F32)
-        wback[side, me] = acc.astype(BF16)
+        wback[side, nearest] = acc.astype(BF16)
         for s in range(1, N):
             d = lax.rem(me + s, N)
-            push(remote(wback.at[side, me], wback.at[side, me], wb_ssem.at[side, s], wb_rsem.at[side, me], where(d)))
+            remote(wback.at[side, nearest], wback.at[side, nearest], wb_ssem.at[side], wb_rsem.at[side], where(d)).start()
 
     def dn_part(m, g):
         return lax.dot_general(g, w_ref[m], (((1,), (1,)), ((), ())), preferred_element_type=F32)
@@ -309,7 +321,7 @@
         nrecv[me] = norm_part
         for s in range(1, N):
             d = lax.rem(me + s, N)
-            push(remote(nrecv.at[me], nrecv.at[me], n_ssem.at[s], n_rsem.at[me], where(d)))
+            remote(nrecv.at[me], nrecv.at[me], n_ssem.at[0], n_rsem.at[0], where(d)).start()
     else:
         norm_ref[...] = norm_part
     dh = dn * gain_ref[...]
@@ -321,19 +333,29 @@
     pair_ref[...] = grad.astype(BF16).reshape(pair_ref.shape)
 
     if fused:
-        collect(0)
-        collect(1)
-        for s in range(1, N):
-            d = lax.rem(me + s, N)
-            remote(nrecv.at[d], nrecv.at[d], n_ssem.at[s], n_rsem.at[d], where(d)).wait_recv()
+
+        @pl.when(is_owner)
+        def _():
+            collect(0)
+            collect(1)
+
+        await_all(nrecv, N - 1, n_ssem.at[0], n_rsem.at[0]).wait()
         acc = nrecv[0]
         for n in range(1, N):
             acc = acc + nrecv[n]
         norm_ref[...] = acc
-        for s in range(1, N):
-            d = lax.rem(me + s, N)
+
+        @pl.when(is_owner)
+        def _():
             for side in range(2):
-                remote(wback.at[side, d], wback.at[side, d], wb_ssem.at[side, s], wb_rsem.at[side, d], where(d)).wait_recv()
+                await_all(wback.at[side], O - 1, ws_ssem.at[side], wb_rsem.at[side]).wait()
+                await_all(wrecv.at[side], N - 1, wb_ssem.at[side], wb_rsem.at[side]).wait_send()
+
+        @pl.when(jnp.logical_not(is_owner))
+        def _():
+            for side in range(2):
+                await_all(wback.at[side], O, ws_ssem.at[side], wb_rsem.at[side]).wait()
+
         wgrad_ref[...] = wback[...].reshape(wgrad_ref.shape)
     for copy in sends:
         copy.wait_send()
@@ -359,8 +381,8 @@
     J = dt.shape[2]
     KH, Z, N = K // 2, C // 2, R * C
     fused = (4 * H) % (16 * N) == 0
-    M = N if fused else 1
-    chunk = 2 * H // N if fused else 8
+    M, O = (N, 2 * R) if fused else (1, 1)
+    chunk = 2 * H // O if fused else 8
     V = pltpu.VMEM
     D = pltpu.SemaphoreType.DMA
     anyspace = pl.BlockSpec(memory_space=pl.ANY)
@@ -394,9 +416,9 @@
             V((T * K, H), F32),
             V((H, T * K), BF16),
             V((T * K, H), F32),
+            V((2, O, chunk, H), BF16),
             V((2, M, chunk, H), BF16),
-            V((2, M, chunk, H), BF16),
-            V((2, M, chunk, H), BF16),
+            V((2, O, chunk, H), BF16),
             V((M, 2, H), F32),
             D((7,)),
             D((2,)),
@@ -408,12 +430,12 @@
             D((Z, 2)),
             D((R, 2)),
             D((R, 2)),
-            D((2, M)),
-            D((2, M)),
-            D((2, M)),
-            D((2, M)),
-            D((M,)),
-            D((M,)),
+            D((2,)),
+            D((2,)),
+            D((2,)),
+            D((2,)),
+            D((1,)),
+            D((1,)),
         ],
         compiler_params=pltpu.CompilerParams(
             collective_id=0, has_side_effects=True, vmem_limit_bytes=56 * 1024 * 1024

time: 31.4 us -> 26.3 us (0.84)
  Pallas kernels: 30.6 us -> 25.6 us
    pallas_call x1, Pallas kernels: 29.8 us -> 24.8 us  [on_device(): pl.pallas_call(functools.partial(kernel, R, C, fused), out_shape=(pltpu.V...]
where the time goes in v3:
time: 26.3 us; the launch traced here: 26.2 us
  Pallas kernels  25.6 us (97%)
  between operations  0.64 us (2%)
    pallas_call x1, Pallas kernels, on_device(): pl.pallas_call(functools.partial(kernel, R, C, fused), out_shape=(pltpu.V...  24.8 us
    pallas_call x1, Pallas kernels, on_device(): pl.pallas_call(finish, out_shape=(jax.ShapeDtypeStruct(z.shape, BF16), ja...  0.76 us

profile of v3, /device:TPU:0, one launch (start us, length us, event | category | flops | bytes accessed | tf_op | source)
XLA Modules:
  0.0 26.2 jit_solution(10157594983848064000)
XLA Ops:
  0.6 24.8 %shard_map.94 = (bf16[1,4,32,128]{3,2,1,0:T(8,128)(2,1)S(1)}, bf16[4,128,128]{2,1,0:T(8,128)(2,1)S(1)}, f32[2,128]{1,0:T(2,128)S(1)}) custom-call(bf16[1,4,32,128]{3,2,1,0:T(8,128)(2,1)} %z_hbm.1, bf16[8,4,16,128]{3,2,1,0:T(8,128)(2,1)} %dt_hbm.1, bf16[1,4,32,128]{3,2,1,0:T(8,128)(2,1)} %a_hbm.1, bf16[1,4,32,128]{3,2,1,0:T(8,128)(2,1)} %b_hbm.1, ...), custom_call_target="tpu_custom_call" | custom-call | tf_op jit(solution)/shard_map/pallas_call | solution.py:390
  25.4 0.8 %shard_map.95 = (bf16[1,4,32,128]{3,2,1,0:T(8,128)(2,1)}, f32[4,128,128]{2,1,0:T(8,128)}, f32[2,128]{1,0:T(2,128)}) custom-call(bf16[1,4,32,128]{3,2,1,0:T(8,128)(2,1)S(1)} %get-tuple-element.6.pair_ref, bf16[4,128,128]{2,1,0:T(8,128)(2,1)S(1)} %get-tuple-element.7.wgrad_ref, f32[2,128]{1,0:T(2,128)S(1)} %get-tuple-element.8.norm_ref), custom_call_target="tpu_custom_call" | custom-call | tf_op jit(solution)/shard_map/pallas_call | solution.py:446

commit v4 on v3

--- a/solution.py
+++ b/solution.py
@@ -124,11 +124,11 @@
         copy.start()
         sends.append(copy)
 
+    for rr in row_peers:
+        for p in range(2):
+            push(remote(b_ref.at[0, :, half(p), :], b_all.at[q, pl.ds(r * T, T)], b_ssem.at[rr, p], b_rsem.at[r, q], (rr, z * 2 + p)))
+    push(remote(b_ref.at[0, :, half(1 - q), :], b_all.at[q, pl.ds(r * T, T)], b_ssem.at[r, 1 - q], b_rsem.at[r, q], (r, other)))
     push(remote(dt_ref, dt_other, dt_sem.at[0], dt_sem.at[1], (r, other)))
-    push(remote(b_ref.at[0, :, half(1 - q), :], b_all.at[q, pl.ds(r * T, T)], b_ssem.at[r, 1 - q], b_rsem.at[r, q], (r, other)))
-    for rr in row_peers:
-        for p in range(2):
-            push(remote(b_ref.at[0, :, half(p), :], b_all.at[q, pl.ds(r * T, T)], b_ssem.at[rr, p], b_rsem.at[r, q], (rr, z * 2 + p)))
     for s in range(1, Z):
         zz = lax.rem(z + s, Z)
         for p in range(2):

time: 26.3 us -> 26.3 us (level)
  no operation moved by 1% of the time
where the time goes in v4:
time: 26.3 us; the launch traced here: 26.2 us
  Pallas kernels  25.6 us (97%)
  between operations  0.64 us (2%)
    pallas_call x1, Pallas kernels, on_device(): pl.pallas_call(functools.partial(kernel, R, C, fused), out_shape=(pltpu.V...  24.8 us
    pallas_call x1, Pallas kernels, on_device(): pl.pallas_call(finish, out_shape=(jax.ShapeDtypeStruct(z.shape, BF16), ja...  0.76 us

profile of v4, /device:TPU:0, one launch (start us, length us, event | category | flops | bytes accessed | tf_op | source)
XLA Modules:
  0.0 26.2 jit_solution(9273292889798392136)
XLA Ops:
  0.6 24.8 %shard_map.94 = (bf16[1,4,32,128]{3,2,1,0:T(8,128)(2,1)S(1)}, bf16[4,128,128]{2,1,0:T(8,128)(2,1)S(1)}, f32[2,128]{1,0:T(2,128)S(1)}) custom-call(bf16[1,4,32,128]{3,2,1,0:T(8,128)(2,1)} %z_hbm.1, bf16[8,4,16,128]{3,2,1,0:T(8,128)(2,1)} %dt_hbm.1, bf16[1,4,32,128]{3,2,1,0:T(8,128)(2,1)} %a_hbm.1, bf16[1,4,32,128]{3,2,1,0:T(8,128)(2,1)} %b_hbm.1, ...), custom_call_target="tpu_custom_call" | custom-call | tf_op jit(solution)/shard_map/pallas_call | solution.py:390
  25.4 0.8 %shard_map.95 = (bf16[1,4,32,128]{3,2,1,0:T(8,128)(2,1)}, f32[4,128,128]{2,1,0:T(8,128)}, f32[2,128]{1,0:T(2,128)}) custom-call(bf16[1,4,32,128]{3,2,1,0:T(8,128)(2,1)S(1)} %get-tuple-element.6.pair_ref, bf16[4,128,128]{2,1,0:T(8,128)(2,1)S(1)} %get-tuple-element.7.wgrad_ref, f32[2,128]{1,0:T(2,128)S(1)} %get-tuple-element.8.norm_ref), custom_call_target="tpu_custom_call" | custom-call | tf_op jit(solution)/shard_map/pallas_call | solution.py:446
